TPU v7x, 32 devices: a whole 2x2x4 slice. The times are simulated.
32 devices in a mesh: inner: 2 (over y), outer: 4 (over z), head: 4 (over x, core).
Axes of the slice: x: 2, y: 2, z: 4, core: 2. Of those that a mesh axis runs over, the one named last changes fastest.
Arguments:
- queries: bfloat16 [2048, 64, 128], P(('inner', 'outer', 'head')), may hold values from -6 to 6
- key_vector_rows: bfloat16 [2048, 8, 128], P(('inner', 'outer'), 'head'), may hold values from -6 to 6
- value_vector_rows: bfloat16 [2048, 8, 128], P(('inner', 'outer'), 'head'), may hold values from -6 to 6
- grad_out: bfloat16 [2048, 64, 128], P(('inner', 'outer', 'head')), may hold values from -24 to 24
Outputs:
- query_grads: bfloat16 [2048, 64, 128], P(('inner', 'outer', 'head'))
- key_gradient_rows: bfloat16 [2048, 8, 128], P(('inner', 'outer'), 'head')
- value_gradient_rows: bfloat16 [2048, 8, 128], P(('inner', 'outer'), 'head')
All inputs are finite; a program needn't handle non-finite values.
Results may differ from a plain program's by a relative error of at most 0.012.
Values may be sent and summed in bfloat16 or wider, within the bound.
No kernel may reach another device: no remote copies, remote signals or barrier semaphores. Data moves between devices by JAX's collectives and lax.ppermute only.
A program may use at most 64 MiB of HBM per device.

v0:
```python
import jax
import jax.numpy as jnp
from jax import lax
from jax.sharding import PartitionSpec as P


def from_behind(value, axis, by):
    peers = lax.axis_size(axis)
    pairs = [(i, i + by) for i in range(peers) if 0 <= i + by < peers]
    return lax.ppermute(value, axis, pairs)


def head_grads(query_part, grad_part, key_part, value_part, allowed):
    softmax_scale = query_part.shape[-1] ** (-0.5)
    scores = (
        jnp.einsum("rgd,kd->grk", query_part, key_part, preferred_element_type=jnp.float32)
        * softmax_scale
    )
    scores = jnp.where(allowed[None], scores, -jnp.inf)
    highest = jnp.max(scores, axis=-1, keepdims=True)
    probs = jnp.exp(scores - highest)
    probs = probs / jnp.sum(probs, axis=-1, keepdims=True)
    probs_low = probs.astype(jnp.bfloat16)
    value_gradient_rows = jnp.einsum(
        "grk,rgd->kd", probs_low, grad_part, preferred_element_type=jnp.float32
    )
    dprobs = jnp.einsum("rgd,kd->grk", grad_part, value_part, preferred_element_type=jnp.float32)
    delta = jnp.sum(probs * dprobs, axis=-1, keepdims=True)
    dscores = (probs * (dprobs - delta)).astype(jnp.bfloat16)
    query_grads = (
        jnp.einsum("grk,kd->rgd", dscores, key_part, preferred_element_type=jnp.float32)
        * softmax_scale
    )
    key_gradient_rows = (
        jnp.einsum("grk,rgd->kd", dscores, query_part, preferred_element_type=jnp.float32)
        * softmax_scale
    )
    return (query_grads, key_gradient_rows, value_gradient_rows)


def block_grads(query_rows, grad_rows, key_window, value_window, allowed):
    row_count, head_count, width = query_rows.shape
    group_count = key_window.shape[1]
    heads_per_group = head_count // group_count
    query_split = query_rows.reshape(row_count, group_count, heads_per_group, width).transpose(
        1, 0, 2, 3
    )
    grad_split = grad_rows.reshape(row_count, group_count, heads_per_group, width).transpose(
        1, 0, 2, 3
    )
    key_split = key_window.transpose(1, 0, 2)
    value_split = value_window.transpose(1, 0, 2)
    query_grads, key_gradient_rows, value_gradient_rows = lax.map(
        lambda packed: head_grads(packed[0], packed[1], packed[2], packed[3], allowed),
        (query_split, grad_split, key_split, value_split),
    )
    query_grads = query_grads.transpose(1, 0, 2, 3).reshape(row_count, head_count, width)
    return (
        query_grads,
        key_gradient_rows.transpose(1, 0, 2),
        value_gradient_rows.transpose(1, 0, 2),
    )


def shards(queries, key_vector_rows, value_vector_rows, grad_out):
    tok_rows = key_vector_rows.shape[0]
    block_index = lax.axis_index(("inner", "outer"))
    query_rows, grad_rows = (
        lax.all_to_all(queries, "head", split_axis=1, concat_axis=0, tiled=True),
        lax.all_to_all(grad_out, "head", split_axis=1, concat_axis=0, tiled=True),
    )
    source = (key_vector_rows, value_vector_rows)
    query_positions = block_index * tok_rows + jnp.arange(tok_rows, dtype=jnp.int32)
    arrived = []
    for shift_by in (2, 1):
        arrived.append(from_behind((source[0], source[1]), ("inner", "outer"), shift_by))
    key_window = jnp.concatenate([arrived[0][0], arrived[1][0], source[0]], axis=0)
    value_window = jnp.concatenate([arrived[0][1], arrived[1][1], source[1]], axis=0)
    key_positions = (block_index - 2) * tok_rows + jnp.arange(3 * tok_rows, dtype=jnp.int32)
    allowed = (key_positions[None, :] <= query_positions[:, None]) & (key_positions[None, :] >= 0)
    query_grads, key_gradient_rows, value_gradient_rows = block_grads(
        query_rows, grad_rows, key_window, value_window, allowed
    )
    query_result = lax.all_to_all(
        query_grads.astype(jnp.bfloat16), "head", split_axis=0, concat_axis=1, tiled=True
    )
    key_slot_rows = key_gradient_rows.reshape(
        3, tok_rows, key_gradient_rows.shape[1], key_gradient_rows.shape[2]
    )
    value_slot_rows = value_gradient_rows.reshape(
        3, tok_rows, value_gradient_rows.shape[1], value_gradient_rows.shape[2]
    )
    key_total = key_slot_rows[2]
    value_total = value_slot_rows[2]
    for back_by in (1, 2):
        key_back, value_back = from_behind(
            (key_slot_rows[2 - back_by], value_slot_rows[2 - back_by]), ("inner", "outer"), -back_by
        )
        key_total = key_total + key_back
        value_total = value_total + value_back
    return (query_result, key_total.astype(jnp.bfloat16), value_total.astype(jnp.bfloat16))


def solution(mesh):
    return jax.shard_map(
        shards,
        mesh=mesh,
        in_specs=(
            P(("inner", "outer", "head"), None, None),
            P(("inner", "outer"), "head", None),
            P(("inner", "outer"), "head", None),
            P(("inner", "outer", "head"), None, None),
        ),
        out_specs=(
            P(("inner", "outer", "head"), None, None),
            P(("inner", "outer"), "head", None),
            P(("inner", "outer"), "head", None),
        ),
        check_vma=False,
    )
```

profile of v0, /device:TPU:0, one launch (start us, length us, event | category | flops | bytes accessed | tf_op | source)
XLA Modules:
  0.0 182.1 jit_solution(10710460803360977241)
XLA Ops:
  0.7 2.9 %copy.51 = bf16[64,64,128]{2,0,1:T(8,128)(2,1)} copy(bf16[64,64,128]{2,1,0:T(8,128)(2,1)} %param.6) | data formatting | bytes 2097152 | tf_op args[0]
  3.6 4.2 %all-to-all-start = ((bf16[64,64,128]{2,0,1:T(8,128)(2,1)}), bf16[64,64,128]{2,0,1:T(8,128)(2,1)S(1)}, u32[]{:S(2)}, u32[]{:S(2)}) async-start(bf16[64,64,128]{2,0,1:T(8,128)(2,1)} %copy.51), calls=%async_computation | async-start | bytes 2097152 | tf_op jit(solution)/shard_map/all_to_all | solution.py:69
  7.8 2.9 %copy.56 = bf16[64,64,128]{2,0,1:T(8,128)(2,1)} copy(bf16[64,64,128]{2,1,0:T(8,128)(2,1)} %param.9) | data formatting | bytes 2097152 | tf_op args[3]
  10.7 11.5 %all-to-all-done = bf16[64,64,128]{2,0,1:T(8,128)(2,1)S(1)} async-done(((bf16[64,64,128]{2,0,1:T(8,128)(2,1)}), bf16[64,64,128]{2,0,1:T(8,128)(2,1)S(1)}, u32[]{:S(2)}, u32[]{:S(2)}) %all-to-all-start) | async-done | bytes 1048608 | tf_op jit(solution)/shard_map/all_to_all | solution.py:69
  22.2 3.5 %all-to-all-start.1 = ((bf16[64,64,128]{2,0,1:T(8,128)(2,1)}), bf16[64,64,128]{2,0,1:T(8,128)(2,1)S(1)}, u32[]{:S(2)}, u32[]{:S(2)}) async-start(bf16[64,64,128]{2,0,1:T(8,128)(2,1)} %copy.56), calls=%async_computation.1 | async-start | bytes 2097152 | tf_op jit(solution)/shard_map/all_to_all | solution.py:70
  25.8 5.2 %collective-permute-start = (bf16[256,2,128]{2,0,1:T(8,128)(2,1)S(1)}, bf16[256,2,128]{2,0,1:T(8,128)(2,1)S(1)}, u32[]{:S(2)}, u32[]{:S(2)}) collective-permute-start(bf16[256,2,128]{2,0,1:T(8,128)(2,1)S(1)} %copy.48), channel_id=1, source_target_pairs={{0,8},{4,12},{8,16},{12,20},{16,24},{20,28},{1,9},{5,13},{9,17},{1... | collective-permute-start | bytes 393224 | tf_op jit(solution)/shard_map/ppermute | solution.py:10
  31.0 3.5 %collective-permute-start.1 = (bf16[256,2,128]{2,0,1:T(8,128)(2,1)S(1)}, bf16[256,2,128]{2,0,1:T(8,128)(2,1)S(1)}, u32[]{:S(2)}, u32[]{:S(2)}) collective-permute-start(bf16[256,2,128]{2,0,1:T(8,128)(2,1)S(1)} %copy.48), channel_id=1, source_target_pairs={{0,4},{4,8},{8,12},{12,16},{16,20},{20,24},{24,28},{1,5},{5,9},{9,... | collective-permute-start | bytes 393224 | tf_op jit(solution)/shard_map/ppermute | solution.py:10
  34.6 3.2 %collective-permute-start.2 = (bf16[256,2,128]{2,0,1:T(8,128)(2,1)S(1)}, bf16[256,2,128]{2,0,1:T(8,128)(2,1)S(1)}, u32[]{:S(2)}, u32[]{:S(2)}) collective-permute-start(bf16[256,2,128]{2,0,1:T(8,128)(2,1)S(1)} %copy.53), channel_id=1, source_target_pairs={{0,8},{4,12},{8,16},{12,20},{16,24},{20,28},{1,9},{5,13},{9,17},{1... | collective-permute-start | bytes 393224 | tf_op jit(solution)/shard_map/ppermute | solution.py:10
  37.8 4.4 %collective-permute-start.3 = (bf16[256,2,128]{2,0,1:T(8,128)(2,1)S(1)}, bf16[256,2,128]{2,0,1:T(8,128)(2,1)S(1)}, u32[]{:S(2)}, u32[]{:S(2)}) collective-permute-start(bf16[256,2,128]{2,0,1:T(8,128)(2,1)S(1)} %copy.53), channel_id=1, source_target_pairs={{0,4},{4,8},{8,12},{12,16},{16,20},{20,24},{24,28},{1,5},{5,9},{9,... | collective-permute-start | bytes 393224 | tf_op jit(solution)/shard_map/ppermute | solution.py:10
  45.9 81.8 %while.15 = (s32[]{:T(128)}, bf16[2,256,8,128]{1,3,2,0:T(8,128)(2,1)}, f32[2,768,128]{2,0,1:T(2,128)}, f32[2,768,128]{2,0,1:T(2,128)}, bf16[2,768,128]{2,1,0:T(8...) while((s32[]{:T(128)}, ...), condition=%wide.region_4.5_spmd.clone, body=%wide.region_0.4_spmd.clone.sunk | while | flops 2034465536 | bytes 100918376 | solution.py:53
  47.0 5.7 %fusion.96 = (f32[8,256]{1,0:T(8,128)S(1)}, f32[8,256,768]{1,2,0:T(8,128)}) fusion(pred[256,768]{0,1:T(8,128)(4,1)S(1)} %compare_and_fusion.2, bf16[2,256,8,128]{3,1,2,0:T(8,128)(2,1)S(1)} %get-tuple-element.218, s32[]{:T(128)} %get-tuple-element.200, bf16[2,768,128]{2,1,0:T(8,128)(2,1)} %get-tuple-element.217), kind=kOutput, calls=%fused_computation.63.clone.1 | convolution fusion | flops 408945408 | bytes 7218176 | tf_op jit(solution)/shard_map/while/body/eval_jaxpr/sub | solution.py:21
  52.6 3.9 %fusion.97 = (f32[8,256]{1,0:T(8,128)S(1)}, f32[768,256,8]{1,0,2:T(8,128)S(1)}) fusion(f32[8,256,768]{1,2,0:T(8,128)} %get-tuple-element.183, f32[8,256]{1,0:T(8,128)S(1)} %get-tuple-element.184, bf16[2,256,8,128]{3,1,2,0:T(8,128)(2,1)S(1)} %copy-done.3, s32[]{:T(128)} %get-tuple-element.200, bf16[2,768,128]{2,1,0:T(8,128)(2,1)S(1)} %get-tuple-element.219), kind=kOutput, calls=%fused_computation.4.clone.1 | convolution fusion | flops 407369728 | bytes 13321216 | tf_op jit(solution)/shard_map/while/body/eval_jaxpr/rgd,kd->grk/dot_general | solution.py:27
  60.4 10.6 %dynamic_update_slice.19 = f32[2,768,128]{2,0,1:T(2,128)} dynamic-update-slice(f32[2,768,128]{2,0,1:T(2,128)} %get-tuple-element.202, f32[1,768,128]{2,0,1:T(1,128)S(1)} %bitcast.141, s32[]{:T(128)} %get-tuple-element.200, s32[]{:T(128)} %constant.13.clone.1..sunk, s32[]{:T(128)} %constant.13.clone.1..sunk) | dynamic-update-slice | bytes 786436 | tf_op jit(solution)/shard_map/while/body/jit(dynamic_update_index_in_dim)/dynamic_update_slice | solution.py:53
  73.3 4.0 %fusion.101 = f32[768,128,1]{1,0,2:T(8,128)S(1)} fusion(bf16[2,256,8,128]{3,1,2,0:T(8,128)(2,1)} %get-tuple-element.220, s32[]{:T(128)} %get-tuple-element.200, f32[8,256,768]{1,2,0:T(8,128)} %get-tuple-element.183, f32[8,256]{1,0:T(8,128)S(1)} %get-tuple-element.184), kind=kOutput, calls=%fused_computation.10.clone.1 | convolution fusion | flops 405798912 | bytes 7217664 | tf_op jit(solution)/shard_map/while/body/eval_jaxpr/grk,rgd->kd/dot_general | solution.py:24
  77.3 8.6 %dynamic_update_slice.20 = f32[2,768,128]{2,0,1:T(2,128)S(1)} dynamic-update-slice(f32[2,768,128]{2,0,1:T(2,128)S(1)} %copy-done.4, f32[1,768,128]{2,0,1:T(1,128)S(1)} %bitcast.143, s32[]{:T(128)} %get-tuple-element.200, s32[]{:T(128)} %constant.13.clone.1..sunk, s32[]{:T(128)} %constant.13.clone.1..sunk) | dynamic-update-slice | bytes 786436 | tf_op jit(solution)/shard_map/while/body/jit(dynamic_update_index_in_dim)/dynamic_update_slice | solution.py:53
  87.9 5.7 %fusion.96 = (f32[8,256]{1,0:T(8,128)S(1)}, f32[8,256,768]{1,2,0:T(8,128)}) fusion(pred[256,768]{0,1:T(8,128)(4,1)S(1)} %compare_and_fusion.2, bf16[2,256,8,128]{3,1,2,0:T(8,128)(2,1)S(1)} %get-tuple-element.218, s32[]{:T(128)} %get-tuple-element.200, bf16[2,768,128]{2,1,0:T(8,128)(2,1)} %get-tuple-element.217), kind=kOutput, calls=%fused_computation.63.clone.1 | convolution fusion | flops 408945408 | bytes 7218176 | tf_op jit(solution)/shard_map/while/body/eval_jaxpr/sub | solution.py:21
  93.5 3.9 %fusion.97 = (f32[8,256]{1,0:T(8,128)S(1)}, f32[768,256,8]{1,0,2:T(8,128)S(1)}) fusion(f32[8,256,768]{1,2,0:T(8,128)} %get-tuple-element.183, f32[8,256]{1,0:T(8,128)S(1)} %get-tuple-element.184, bf16[2,256,8,128]{3,1,2,0:T(8,128)(2,1)S(1)} %copy-done.3, s32[]{:T(128)} %get-tuple-element.200, bf16[2,768,128]{2,1,0:T(8,128)(2,1)S(1)} %get-tuple-element.219), kind=kOutput, calls=%fused_computation.4.clone.1 | convolution fusion | flops 407369728 | bytes 13321216 | tf_op jit(solution)/shard_map/while/body/eval_jaxpr/rgd,kd->grk/dot_general | solution.py:27
  101.3 10.6 %dynamic_update_slice.19 = f32[2,768,128]{2,0,1:T(2,128)} dynamic-update-slice(f32[2,768,128]{2,0,1:T(2,128)} %get-tuple-element.202, f32[1,768,128]{2,0,1:T(1,128)S(1)} %bitcast.141, s32[]{:T(128)} %get-tuple-element.200, s32[]{:T(128)} %constant.13.clone.1..sunk, s32[]{:T(128)} %constant.13.clone.1..sunk) | dynamic-update-slice | bytes 786436 | tf_op jit(solution)/shard_map/while/body/jit(dynamic_update_index_in_dim)/dynamic_update_slice | solution.py:53
  114.2 4.0 %fusion.101 = f32[768,128,1]{1,0,2:T(8,128)S(1)} fusion(bf16[2,256,8,128]{3,1,2,0:T(8,128)(2,1)} %get-tuple-element.220, s32[]{:T(128)} %get-tuple-element.200, f32[8,256,768]{1,2,0:T(8,128)} %get-tuple-element.183, f32[8,256]{1,0:T(8,128)S(1)} %get-tuple-element.184), kind=kOutput, calls=%fused_computation.10.clone.1 | convolution fusion | flops 405798912 | bytes 7217664 | tf_op jit(solution)/shard_map/while/body/eval_jaxpr/grk,rgd->kd/dot_general | solution.py:24
  118.2 8.6 %dynamic_update_slice.20 = f32[2,768,128]{2,0,1:T(2,128)S(1)} dynamic-update-slice(f32[2,768,128]{2,0,1:T(2,128)S(1)} %copy-done.4, f32[1,768,128]{2,0,1:T(1,128)S(1)} %bitcast.143, s32[]{:T(128)} %get-tuple-element.200, s32[]{:T(128)} %constant.13.clone.1..sunk, s32[]{:T(128)} %constant.13.clone.1..sunk) | dynamic-update-slice | bytes 786436 | tf_op jit(solution)/shard_map/while/body/jit(dynamic_update_index_in_dim)/dynamic_update_slice | solution.py:53
  130.3 3.5 %all-to-all-start.2 = ((bf16[256,16,128]{2,1,0:T(8,128)(2,1)}), bf16[256,16,128]{2,1,0:T(8,128)(2,1)S(1)}, u32[]{:S(2)}, u32[]{:S(2)}) async-start(bf16[256,16,128]{2,1,0:T(8,128)(2,1)} %bitcast.11), calls=%async_computation.2 | async-start | bytes 2097152 | tf_op jit(solution)/shard_map/all_to_all | solution.py:84
  141.1 8.1 %collective-permute-done.6 = f32[256,2,128]{2,1,0:T(2,128)S(1)} collective-permute-done((f32[256,2,128]{2,1,0:T(2,128)S(1)}, f32[256,2,128]{2,1,0:T(2,128)S(1)}, u32[]{:S(2)}, u32[]{:S(2)}) %collective-permute-start.6) | collective-permute-done | bytes 262176 | tf_op jit(solution)/shard_map/ppermute | solution.py:10
  149.2 13.1 %collective-permute-done.7 = f32[256,2,128]{2,1,0:T(2,128)S(1)} collective-permute-done((f32[256,2,128]{2,1,0:T(2,128)S(1)}, f32[256,2,128]{2,1,0:T(2,128)S(1)}, u32[]{:S(2)}, u32[]{:S(2)}) %collective-permute-start.7) | collective-permute-done | bytes 262176 | tf_op jit(solution)/shard_map/ppermute | solution.py:10
  164.1 14.8 %collective-permute-done.5 = f32[256,2,128]{2,1,0:T(2,128)S(1)} collective-permute-done((f32[256,2,128]{2,1,0:T(2,128)S(1)}, f32[256,2,128]{2,1,0:T(2,128)S(1)}, u32[]{:S(2)}, u32[]{:S(2)}) %collective-permute-start.5) | collective-permute-done | bytes 262176 | tf_op jit(solution)/shard_map/ppermute | solution.py:10
  (73 shorter events, 34.8 us)
Async XLA Ops:
  0.6 25.1 %copy-start.8 = (bf16[256,2,128]{2,1,0:T(2,128)(2,1)S(1)}, bf16[256,2,128]{2,1,0:T(2,128)(2,1)}, u32[]{:S(2)}) copy-start(bf16[256,2,128]{2,1,0:T(2,128)(2,1)} %param.7) | copy-start | bytes 393220
  0.6 33.9 %copy-start.9 = (bf16[256,2,128]{2,1,0:T(2,128)(2,1)S(1)}, bf16[256,2,128]{2,1,0:T(2,128)(2,1)}, u32[]{:S(2)}) copy-start(bf16[256,2,128]{2,1,0:T(2,128)(2,1)} %param.8) | copy-start | bytes 393220
  3.6 18.7 %all-to-all-start = ((bf16[64,64,128]{2,0,1:T(8,128)(2,1)}), bf16[64,64,128]{2,0,1:T(8,128)(2,1)S(1)}, u32[]{:S(2)}, u32[]{:S(2)}) async-start(bf16[64,64,128]{2,0,1:T(8,128)(2,1)} %copy.51), calls=%async_computation | async-start | bytes 2097152 | tf_op jit(solution)/shard_map/all_to_all | solution.py:69
  22.2 22.6 %all-to-all-start.1 = ((bf16[64,64,128]{2,0,1:T(8,128)(2,1)}), bf16[64,64,128]{2,0,1:T(8,128)(2,1)S(1)}, u32[]{:S(2)}, u32[]{:S(2)}) async-start(bf16[64,64,128]{2,0,1:T(8,128)(2,1)} %copy.56), calls=%async_computation.1 | async-start | bytes 2097152 | tf_op jit(solution)/shard_map/all_to_all | solution.py:70
  25.8 17.0 %collective-permute-start = (bf16[256,2,128]{2,0,1:T(8,128)(2,1)S(1)}, bf16[256,2,128]{2,0,1:T(8,128)(2,1)S(1)}, u32[]{:S(2)}, u32[]{:S(2)}) collective-permute-start(bf16[256,2,128]{2,0,1:T(8,128)(2,1)S(1)} %copy.48), channel_id=1, source_target_pairs={{0,8},{4,12},{8,16},{12,20},{16,24},{20,28},{1,9},{5,13},{9,17},{1... | collective-permute-start | bytes 393224 | tf_op jit(solution)/shard_map/ppermute | solution.py:10
  31.0 11.7 %collective-permute-start.1 = (bf16[256,2,128]{2,0,1:T(8,128)(2,1)S(1)}, bf16[256,2,128]{2,0,1:T(8,128)(2,1)S(1)}, u32[]{:S(2)}, u32[]{:S(2)}) collective-permute-start(bf16[256,2,128]{2,0,1:T(8,128)(2,1)S(1)} %copy.48), channel_id=1, source_target_pairs={{0,4},{4,8},{8,12},{12,16},{16,20},{20,24},{24,28},{1,5},{5,9},{9,... | collective-permute-start | bytes 393224 | tf_op jit(solution)/shard_map/ppermute | solution.py:10
  34.6 9.0 %collective-permute-start.2 = (bf16[256,2,128]{2,0,1:T(8,128)(2,1)S(1)}, bf16[256,2,128]{2,0,1:T(8,128)(2,1)S(1)}, u32[]{:S(2)}, u32[]{:S(2)}) collective-permute-start(bf16[256,2,128]{2,0,1:T(8,128)(2,1)S(1)} %copy.53), channel_id=1, source_target_pairs={{0,8},{4,12},{8,16},{12,20},{16,24},{20,28},{1,9},{5,13},{9,17},{1... | collective-permute-start | bytes 393224 | tf_op jit(solution)/shard_map/ppermute | solution.py:10
  37.8 6.9 %collective-permute-start.3 = (bf16[256,2,128]{2,0,1:T(8,128)(2,1)S(1)}, bf16[256,2,128]{2,0,1:T(8,128)(2,1)S(1)}, u32[]{:S(2)}, u32[]{:S(2)}) collective-permute-start(bf16[256,2,128]{2,0,1:T(8,128)(2,1)S(1)} %copy.53), channel_id=1, source_target_pairs={{0,4},{4,8},{8,12},{12,16},{16,20},{20,24},{24,28},{1,5},{5,9},{9,... | collective-permute-start | bytes 393224 | tf_op jit(solution)/shard_map/ppermute | solution.py:10
  45.9 10.7 %copy-start.1 = (bf16[2,256,8,128]{3,1,2,0:T(8,128)(2,1)}, bf16[2,256,8,128]{3,1,2,0:T(8,128)(2,1)S(1)}, u32[]{:S(2)}) copy-start(bf16[2,256,8,128]{3,1,2,0:T(8,128)(2,1)S(1)} %get-tuple-element.218) | copy-start | bytes 3145732 | tf_op jit(solution)/shard_map/while
  45.9 10.7 %copy-start.6 = (bf16[2,768,128]{2,1,0:T(8,128)(2,1)}, bf16[2,768,128]{2,1,0:T(8,128)(2,1)S(1)}, u32[]{:S(2)}) copy-start(bf16[2,768,128]{2,1,0:T(8,128)(2,1)S(1)} %get-tuple-element.219) | copy-start | bytes 1179652 | tf_op jit(solution)/shard_map/while
  45.9 6.7 %copy-start.3 = (bf16[2,256,8,128]{3,1,2,0:T(8,128)(2,1)S(1)}, bf16[2,256,8,128]{3,1,2,0:T(8,128)(2,1)}, u32[]{:S(2)}) copy-start(bf16[2,256,8,128]{3,1,2,0:T(8,128)(2,1)} %get-tuple-element.220) | copy-start | bytes 3145732 | tf_op jit(solution)/shard_map/while
  52.6 4.6 %copy-start = (f32[8,256,768]{1,2,0:T(8,128)S(1)}, f32[8,256,768]{1,2,0:T(8,128)}, u32[]{:S(2)}) copy-start(f32[8,256,768]{1,2,0:T(8,128)} %get-tuple-element.183) | copy-start | bytes 18874372 | tf_op jit(solution)/shard_map/while
  73.3 13.4 %copy-start.2 = (bf16[2,256,8,128]{3,1,2,0:T(8,128)(2,1)S(1)}, bf16[2,256,8,128]{3,1,2,0:T(8,128)(2,1)}, u32[]{:S(2)}) copy-start(bf16[2,256,8,128]{3,1,2,0:T(8,128)(2,1)} %copy-done.1) | copy-start | bytes 3145732 | tf_op jit(solution)/shard_map/while
  73.3 13.4 %copy-start.7 = (bf16[2,768,128]{2,1,0:T(8,128)(2,1)S(1)}, bf16[2,768,128]{2,1,0:T(8,128)(2,1)}, u32[]{:S(2)}) copy-start(bf16[2,768,128]{2,1,0:T(8,128)(2,1)} %copy-done.6) | copy-start | bytes 1179652 | tf_op jit(solution)/shard_map/while
  86.8 10.7 %copy-start.1 = (bf16[2,256,8,128]{3,1,2,0:T(8,128)(2,1)}, bf16[2,256,8,128]{3,1,2,0:T(8,128)(2,1)S(1)}, u32[]{:S(2)}) copy-start(bf16[2,256,8,128]{3,1,2,0:T(8,128)(2,1)S(1)} %get-tuple-element.218) | copy-start | bytes 3145732 | tf_op jit(solution)/shard_map/while
  86.8 10.7 %copy-start.6 = (bf16[2,768,128]{2,1,0:T(8,128)(2,1)}, bf16[2,768,128]{2,1,0:T(8,128)(2,1)S(1)}, u32[]{:S(2)}) copy-start(bf16[2,768,128]{2,1,0:T(8,128)(2,1)S(1)} %get-tuple-element.219) | copy-start | bytes 1179652 | tf_op jit(solution)/shard_map/while
  86.8 6.7 %copy-start.3 = (bf16[2,256,8,128]{3,1,2,0:T(8,128)(2,1)S(1)}, bf16[2,256,8,128]{3,1,2,0:T(8,128)(2,1)}, u32[]{:S(2)}) copy-start(bf16[2,256,8,128]{3,1,2,0:T(8,128)(2,1)} %get-tuple-element.220) | copy-start | bytes 3145732 | tf_op jit(solution)/shard_map/while
  114.2 13.4 %copy-start.2 = (bf16[2,256,8,128]{3,1,2,0:T(8,128)(2,1)S(1)}, bf16[2,256,8,128]{3,1,2,0:T(8,128)(2,1)}, u32[]{:S(2)}) copy-start(bf16[2,256,8,128]{3,1,2,0:T(8,128)(2,1)} %copy-done.1) | copy-start | bytes 3145732 | tf_op jit(solution)/shard_map/while
  114.2 13.4 %copy-start.7 = (bf16[2,768,128]{2,1,0:T(8,128)(2,1)S(1)}, bf16[2,768,128]{2,1,0:T(8,128)(2,1)}, u32[]{:S(2)}) copy-start(bf16[2,768,128]{2,1,0:T(8,128)(2,1)} %copy-done.6) | copy-start | bytes 1179652 | tf_op jit(solution)/shard_map/while
  130.3 50.5 %all-to-all-start.2 = ((bf16[256,16,128]{2,1,0:T(8,128)(2,1)}), bf16[256,16,128]{2,1,0:T(8,128)(2,1)S(1)}, u32[]{:S(2)}, u32[]{:S(2)}) async-start(bf16[256,16,128]{2,1,0:T(8,128)(2,1)} %bitcast.11), calls=%async_computation.2 | async-start | bytes 2097152 | tf_op jit(solution)/shard_map/all_to_all | solution.py:84
  134.9 14.3 %collective-permute-start.6 = (f32[256,2,128]{2,1,0:T(2,128)S(1)}, f32[256,2,128]{2,1,0:T(2,128)S(1)}, u32[]{:S(2)}, u32[]{:S(2)}) collective-permute-start(f32[256,2,128]{2,1,0:T(2,128)S(1)} %get-tuple-element.108), channel_id=1, source_target_pairs={{4,0},{8,4},{12,8},{16,12},{20,16},{24,20},{28,24},{5,1},{9,5},{13... | collective-permute-start | bytes 786440 | tf_op jit(solution)/shard_map/ppermute | solution.py:10
  136.2 26.2 %collective-permute-start.7 = (f32[256,2,128]{2,1,0:T(2,128)S(1)}, f32[256,2,128]{2,1,0:T(2,128)S(1)}, u32[]{:S(2)}, u32[]{:S(2)}) collective-permute-start(f32[256,2,128]{2,1,0:T(2,128)S(1)} %get-tuple-element.109), channel_id=1, source_target_pairs={{8,0},{12,4},{16,8},{20,12},{24,16},{28,20},{9,1},{13,5},{17,9},{2... | collective-permute-start | bytes 786440 | tf_op jit(solution)/shard_map/ppermute | solution.py:10
  138.5 25.6 %collective-permute-start.4 = (f32[256,2,128]{2,1,0:T(2,128)S(1)}, f32[256,2,128]{2,1,0:T(2,128)S(1)}, u32[]{:S(2)}, u32[]{:S(2)}) collective-permute-start(f32[256,2,128]{2,1,0:T(2,128)S(1)} %get-tuple-element.110), channel_id=1, source_target_pairs={{4,0},{8,4},{12,8},{16,12},{20,16},{24,20},{28,24},{5,1},{9,5},{13... | collective-permute-start | bytes 786440 | tf_op jit(solution)/shard_map/ppermute | solution.py:10
  139.8 39.1 %collective-permute-start.5 = (f32[256,2,128]{2,1,0:T(2,128)S(1)}, f32[256,2,128]{2,1,0:T(2,128)S(1)}, u32[]{:S(2)}, u32[]{:S(2)}) collective-permute-start(f32[256,2,128]{2,1,0:T(2,128)S(1)} %get-tuple-element.111), channel_id=1, source_target_pairs={{8,0},{12,4},{16,8},{20,12},{24,16},{28,20},{9,1},{13,5},{17,9},{2... | collective-permute-start | bytes 786440 | tf_op jit(solution)/shard_map/ppermute | solution.py:10
  (5 other events, 14.3 us)
where the time goes:
time: 184 us; the launch traced here: 182 us
  local copies, waits for them, and re-layouts  54.4 us (30%)
  waiting for transfers between devices  48.7 us (26%)
  matrix products  35.8 us (19%)
  starting transfers between devices  32.7 us (18%)
  other arithmetic  9.45 us (5%)
    dynamic_update_slice x4, local copies, waits for them, and re-layouts, block_grads(): lax.map(lambda packed: head_grads(packed[0], packed[1], packed[2], packed...  38.2 us
    ppermute x8, waiting for transfers between devices, from_behind(): return lax.ppermute(value, axis, pairs)  37.1 us
    ppermute x8, starting transfers between devices, from_behind(): return lax.ppermute(value, axis, pairs)  21.5 us
    all_to_all x1, waiting for transfers between devices, shards(): lax.all_to_all(queries, 'head', split_axis=1, concat_axis=0, tiled=True)  11.5 us
    sub x2, matrix products, head_grads(): probs = jnp.exp(scores - highest)  11.3 us
    dot_general x2, matrix products, head_grads(): jnp.einsum('grk,rgd->kd', probs_low, grad_part, preferred_element_type=jn...  7.94 us
    dot_general x2, matrix products, head_grads(): jnp.einsum('rgd,kd->grk', grad_part, value_part, preferred_element_type=j...  7.84 us
    unnamed x8, local copies, waits for them, and re-layouts  5.86 us
  transfers between devices with their start and end apart: 11, of which 5 were waited for; matrix products, arithmetic and copies ran while one was open for 6% of the time, Pallas kernels for 0%

commit v1 on v0

--- a/solution.py
+++ b/solution.py
@@ -65,8 +65,20 @@
 def shards(queries, key_vector_rows, value_vector_rows, grad_out):
     tok_rows = key_vector_rows.shape[0]
     block_index = lax.axis_index(("inner", "outer"))
+
+    def treat_rounds_all(t0):
+        return jnp.concatenate(
+            jax.lax.all_to_all(
+                jnp.stack(jnp.split(t0, jax.lax.axis_size("head"), axis=1)),
+                axis_name="head",
+                split_axis=0,
+                concat_axis=0,
+            ),
+            axis=0,
+        )
+
     query_rows, grad_rows = (
-        lax.all_to_all(queries, "head", split_axis=1, concat_axis=0, tiled=True),
+        treat_rounds_all(queries),
         lax.all_to_all(grad_out, "head", split_axis=1, concat_axis=0, tiled=True),
     )
     source = (key_vector_rows, value_vector_rows)

time: 184 us -> 184 us (level)
  local copies, waits for them, and re-layouts: 54.4 us -> 52 us
    all_to_all x1, waiting for transfers between devices: 0.01 us -> 11.9 us  [shards(): lax.all_to_all(grad_out, 'head', split_axis=1, concat_axis=0, tiled=True)]
    all_to_all x1, waiting for transfers between devices: 11.5 us -> 0.01 us  [treat_rounds_all(): jax.lax.all_to_all(jnp.stack(jnp.split(t0, jax.lax.axis_size('head'), axi...]
    unnamed x8 -> x7, local copies, waits for them, and re-layouts: 5.86 us -> 2.96 us
where the time goes in v1:
time: 184 us; the launch traced here: 182 us
  local copies, waits for them, and re-layouts  52 us (28%)
  waiting for transfers between devices  49.1 us (27%)
  matrix products  36 us (20%)
  starting transfers between devices  32.7 us (18%)
  other arithmetic  11.2 us (6%)
    dynamic_update_slice x4, local copies, waits for them, and re-layouts, block_grads(): lax.map(lambda packed: head_grads(packed[0], packed[1], packed[2], packed...  38.2 us
    ppermute x8, waiting for transfers between devices, from_behind(): return lax.ppermute(value, axis, pairs)  37.2 us
    ppermute x8, starting transfers between devices, from_behind(): return lax.ppermute(value, axis, pairs)  21.5 us
    all_to_all x1, waiting for transfers between devices, shards(): lax.all_to_all(grad_out, 'head', split_axis=1, concat_axis=0, tiled=True)  11.9 us
    sub x2, matrix products, head_grads(): probs = jnp.exp(scores - highest)  11.3 us
    dot_general x2, matrix products, head_grads(): jnp.einsum('rgd,kd->grk', grad_part, value_part, preferred_element_type=j...  8.04 us
    dot_general x2, matrix products, head_grads(): jnp.einsum('grk,rgd->kd', probs_low, grad_part, preferred_element_type=jn...  7.95 us
    dot_general x2, matrix products, head_grads(): jnp.einsum('grk,kd->rgd', dscores, key_part, preferred_element_type=jnp.f...  4.66 us
  transfers between devices with their start and end apart: 11, of which 5 were waited for; matrix products, arithmetic and copies ran while one was open for 6% of the time, Pallas kernels for 0%

profile of v1, /device:TPU:0, one launch (start us, length us, event | category | flops | bytes accessed | tf_op | source)
XLA Modules:
  0.0 182.1 jit_solution(11861679983969731441)
XLA Ops:
  0.7 2.9 %copy.55 = bf16[64,64,128]{2,0,1:T(8,128)(2,1)} copy(bf16[64,64,128]{2,1,0:T(8,128)(2,1)} %param.9) | data formatting | bytes 2097152 | tf_op args[3]
  3.6 4.2 %all-to-all-start.1 = ((bf16[64,64,128]{2,0,1:T(8,128)(2,1)}), bf16[64,64,128]{2,0,1:T(8,128)(2,1)S(1)}, u32[]{:S(2)}, u32[]{:S(2)}) async-start(bf16[64,64,128]{2,0,1:T(8,128)(2,1)} %copy.55), calls=%async_computation.1 | async-start | bytes 2097152 | tf_op jit(solution)/shard_map/all_to_all | solution.py:82
  10.3 11.9 %all-to-all-done.1 = bf16[64,64,128]{2,0,1:T(8,128)(2,1)S(1)} async-done(((bf16[64,64,128]{2,0,1:T(8,128)(2,1)}), bf16[64,64,128]{2,0,1:T(8,128)(2,1)S(1)}, u32[]{:S(2)}, u32[]{:S(2)}) %all-to-all-start.1) | async-done | bytes 1048608 | tf_op jit(solution)/shard_map/all_to_all | solution.py:82
  22.2 3.5 %all-to-all-start = ((bf16[4,64,16,128]{3,2,1,0:T(8,128)(2,1)}), bf16[4,64,16,128]{3,2,1,0:T(8,128)(2,1)S(1)}, u32[]{:S(2)}, u32[]{:S(2)}) async-start(bf16[4,64,16,128]{3,2,1,0:T(8,128)(2,1)} %pad_maximum_fusion), calls=%async_computation | async-start | bytes 2097152 | tf_op jit(solution)/shard_map/all_to_all | solution.py:71
  25.8 5.2 %collective-permute-start = (bf16[256,2,128]{2,0,1:T(8,128)(2,1)S(1)}, bf16[256,2,128]{2,0,1:T(8,128)(2,1)S(1)}, u32[]{:S(2)}, u32[]{:S(2)}) collective-permute-start(bf16[256,2,128]{2,0,1:T(8,128)(2,1)S(1)} %copy.48), channel_id=1, source_target_pairs={{0,8},{4,12},{8,16},{12,20},{16,24},{20,28},{1,9},{5,13},{9,17},{1... | collective-permute-start | bytes 393224 | tf_op jit(solution)/shard_map/ppermute | solution.py:10
  31.0 3.5 %collective-permute-start.1 = (bf16[256,2,128]{2,0,1:T(8,128)(2,1)S(1)}, bf16[256,2,128]{2,0,1:T(8,128)(2,1)S(1)}, u32[]{:S(2)}, u32[]{:S(2)}) collective-permute-start(bf16[256,2,128]{2,0,1:T(8,128)(2,1)S(1)} %copy.48), channel_id=1, source_target_pairs={{0,4},{4,8},{8,12},{12,16},{16,20},{20,24},{24,28},{1,5},{5,9},{9,... | collective-permute-start | bytes 393224 | tf_op jit(solution)/shard_map/ppermute | solution.py:10
  34.6 3.2 %collective-permute-start.2 = (bf16[256,2,128]{2,0,1:T(8,128)(2,1)S(1)}, bf16[256,2,128]{2,0,1:T(8,128)(2,1)S(1)}, u32[]{:S(2)}, u32[]{:S(2)}) collective-permute-start(bf16[256,2,128]{2,0,1:T(8,128)(2,1)S(1)} %copy.52), channel_id=1, source_target_pairs={{0,8},{4,12},{8,16},{12,20},{16,24},{20,28},{1,9},{5,13},{9,17},{1... | collective-permute-start | bytes 393224 | tf_op jit(solution)/shard_map/ppermute | solution.py:10
  37.8 4.4 %collective-permute-start.3 = (bf16[256,2,128]{2,0,1:T(8,128)(2,1)S(1)}, bf16[256,2,128]{2,0,1:T(8,128)(2,1)S(1)}, u32[]{:S(2)}, u32[]{:S(2)}) collective-permute-start(bf16[256,2,128]{2,0,1:T(8,128)(2,1)S(1)} %copy.52), channel_id=1, source_target_pairs={{0,4},{4,8},{8,12},{12,16},{16,20},{20,24},{24,28},{1,5},{5,9},{9,... | collective-permute-start | bytes 393224 | tf_op jit(solution)/shard_map/ppermute | solution.py:10
  45.8 81.8 %while.15 = (s32[]{:T(128)}, bf16[2,256,8,128]{1,3,2,0:T(8,128)(2,1)}, f32[2,768,128]{2,0,1:T(2,128)}, f32[2,768,128]{2,0,1:T(2,128)}, bf16[2,768,128]{2,1,0:T(8...) while((s32[]{:T(128)}, ...), condition=%wide.region_4.5_spmd.clone, body=%wide.region_0.4_spmd.clone.sunk | while | flops 2034465536 | bytes 101966936 | solution.py:53
  46.9 5.6 %fusion.96 = (f32[8,256]{1,0:T(8,128)S(1)}, f32[8,256,768]{1,2,0:T(8,128)}) fusion(pred[256,768]{0,1:T(8,128)(4,1)S(1)} %compare_and_fusion.2, bf16[2,256,8,128]{3,1,2,0:T(8,128)(2,1)S(1)} %get-tuple-element.222, s32[]{:T(128)} %get-tuple-element.204, bf16[2,768,128]{2,1,0:T(8,128)(2,1)} %get-tuple-element.221), kind=kOutput, calls=%fused_computation.68.clone.1 | convolution fusion | flops 408945408 | bytes 7218176 | tf_op jit(solution)/shard_map/while/body/eval_jaxpr/sub | solution.py:21
  52.5 4.0 %fusion.97 = (f32[8,256]{1,0:T(8,128)S(1)}, f32[768,256,8]{1,0,2:T(8,128)S(1)}) fusion(f32[8,256,768]{1,2,0:T(8,128)} %get-tuple-element.187, f32[8,256]{1,0:T(8,128)S(1)} %get-tuple-element.188, bf16[2,256,8,128]{3,1,2,0:T(8,128)(2,1)S(1)} %get-tuple-element.224, s32[]{:T(128)} %get-tuple-element.204, bf16[2,768,128]{2,1,0:T(8,128)(2,1)} %get-tuple-element.223), kind=kOutput, calls=%fused_computation.4.clone.1 | convolution fusion | flops 407369728 | bytes 13321216 | tf_op jit(solution)/shard_map/while/body/eval_jaxpr/rgd,kd->grk/dot_general | solution.py:27
  60.4 10.6 %dynamic_update_slice.19 = f32[2,768,128]{2,0,1:T(2,128)} dynamic-update-slice(f32[2,768,128]{2,0,1:T(2,128)} %get-tuple-element.206, f32[1,768,128]{2,0,1:T(1,128)S(1)} %bitcast.146, s32[]{:T(128)} %get-tuple-element.204, s32[]{:T(128)} %constant.13.clone.1..sunk, s32[]{:T(128)} %constant.13.clone.1..sunk) | dynamic-update-slice | bytes 786436 | tf_op jit(solution)/shard_map/while/body/jit(dynamic_update_index_in_dim)/dynamic_update_slice | solution.py:53
  73.3 4.0 %fusion.101 = f32[768,128,1]{1,0,2:T(8,128)S(1)} fusion(bf16[2,256,8,128]{3,1,2,0:T(8,128)(2,1)} %copy-done.3, s32[]{:T(128)} %get-tuple-element.204, f32[8,256,768]{1,2,0:T(8,128)} %get-tuple-element.187, f32[8,256]{1,0:T(8,128)S(1)} %get-tuple-element.188), kind=kOutput, calls=%fused_computation.10.clone.1 | convolution fusion | flops 405798912 | bytes 7217664 | tf_op jit(solution)/shard_map/while/body/eval_jaxpr/grk,rgd->kd/dot_general | solution.py:24
  77.3 8.6 %dynamic_update_slice.20 = f32[2,768,128]{2,0,1:T(2,128)S(1)} dynamic-update-slice(f32[2,768,128]{2,0,1:T(2,128)S(1)} %copy-done.5, f32[1,768,128]{2,0,1:T(1,128)S(1)} %bitcast.148, s32[]{:T(128)} %get-tuple-element.204, s32[]{:T(128)} %constant.13.clone.1..sunk, s32[]{:T(128)} %constant.13.clone.1..sunk) | dynamic-update-slice | bytes 786436 | tf_op jit(solution)/shard_map/while/body/jit(dynamic_update_index_in_dim)/dynamic_update_slice | solution.py:53
  87.8 5.7 %fusion.96 = (f32[8,256]{1,0:T(8,128)S(1)}, f32[8,256,768]{1,2,0:T(8,128)}) fusion(pred[256,768]{0,1:T(8,128)(4,1)S(1)} %compare_and_fusion.2, bf16[2,256,8,128]{3,1,2,0:T(8,128)(2,1)S(1)} %get-tuple-element.222, s32[]{:T(128)} %get-tuple-element.204, bf16[2,768,128]{2,1,0:T(8,128)(2,1)} %get-tuple-element.221), kind=kOutput, calls=%fused_computation.68.clone.1 | convolution fusion | flops 408945408 | bytes 7218176 | tf_op jit(solution)/shard_map/while/body/eval_jaxpr/sub | solution.py:21
  93.4 4.0 %fusion.97 = (f32[8,256]{1,0:T(8,128)S(1)}, f32[768,256,8]{1,0,2:T(8,128)S(1)}) fusion(f32[8,256,768]{1,2,0:T(8,128)} %get-tuple-element.187, f32[8,256]{1,0:T(8,128)S(1)} %get-tuple-element.188, bf16[2,256,8,128]{3,1,2,0:T(8,128)(2,1)S(1)} %get-tuple-element.224, s32[]{:T(128)} %get-tuple-element.204, bf16[2,768,128]{2,1,0:T(8,128)(2,1)} %get-tuple-element.223), kind=kOutput, calls=%fused_computation.4.clone.1 | convolution fusion | flops 407369728 | bytes 13321216 | tf_op jit(solution)/shard_map/while/body/eval_jaxpr/rgd,kd->grk/dot_general | solution.py:27
  101.3 10.6 %dynamic_update_slice.19 = f32[2,768,128]{2,0,1:T(2,128)} dynamic-update-slice(f32[2,768,128]{2,0,1:T(2,128)} %get-tuple-element.206, f32[1,768,128]{2,0,1:T(1,128)S(1)} %bitcast.146, s32[]{:T(128)} %get-tuple-element.204, s32[]{:T(128)} %constant.13.clone.1..sunk, s32[]{:T(128)} %constant.13.clone.1..sunk) | dynamic-update-slice | bytes 786436 | tf_op jit(solution)/shard_map/while/body/jit(dynamic_update_index_in_dim)/dynamic_update_slice | solution.py:53
  114.2 4.0 %fusion.101 = f32[768,128,1]{1,0,2:T(8,128)S(1)} fusion(bf16[2,256,8,128]{3,1,2,0:T(8,128)(2,1)} %copy-done.3, s32[]{:T(128)} %get-tuple-element.204, f32[8,256,768]{1,2,0:T(8,128)} %get-tuple-element.187, f32[8,256]{1,0:T(8,128)S(1)} %get-tuple-element.188), kind=kOutput, calls=%fused_computation.10.clone.1 | convolution fusion | flops 405798912 | bytes 7217664 | tf_op jit(solution)/shard_map/while/body/eval_jaxpr/grk,rgd->kd/dot_general | solution.py:24
  118.2 8.6 %dynamic_update_slice.20 = f32[2,768,128]{2,0,1:T(2,128)S(1)} dynamic-update-slice(f32[2,768,128]{2,0,1:T(2,128)S(1)} %copy-done.5, f32[1,768,128]{2,0,1:T(1,128)S(1)} %bitcast.148, s32[]{:T(128)} %get-tuple-element.204, s32[]{:T(128)} %constant.13.clone.1..sunk, s32[]{:T(128)} %constant.13.clone.1..sunk) | dynamic-update-slice | bytes 786436 | tf_op jit(solution)/shard_map/while/body/jit(dynamic_update_index_in_dim)/dynamic_update_slice | solution.py:53
  127.6 2.6 %copy.57 = bf16[256,2,8,128]{3,2,1,0:T(8,128)(2,1)} copy(bf16[256,2,8,128]{0,3,2,1:T(8,128)(2,1)} %bitcast.152) | data formatting | bytes 2097152 | tf_op jit(solution)/shard_map/convert_element_type | solution.py:97
  130.3 3.5 %all-to-all-start.2 = ((bf16[256,16,128]{2,1,0:T(8,128)(2,1)}), bf16[256,16,128]{2,1,0:T(8,128)(2,1)S(1)}, u32[]{:S(2)}, u32[]{:S(2)}) async-start(bf16[256,16,128]{2,1,0:T(8,128)(2,1)} %bitcast.13), calls=%async_computation.2 | async-start | bytes 2097152 | tf_op jit(solution)/shard_map/all_to_all | solution.py:96
  141.1 8.1 %collective-permute-done.6 = f32[256,2,128]{2,1,0:T(2,128)S(1)} collective-permute-done((f32[256,2,128]{2,1,0:T(2,128)S(1)}, f32[256,2,128]{2,1,0:T(2,128)S(1)}, u32[]{:S(2)}, u32[]{:S(2)}) %collective-permute-start.6) | collective-permute-done | bytes 262176 | tf_op jit(solution)/shard_map/ppermute | solution.py:10
  149.2 13.1 %collective-permute-done.7 = f32[256,2,128]{2,1,0:T(2,128)S(1)} collective-permute-done((f32[256,2,128]{2,1,0:T(2,128)S(1)}, f32[256,2,128]{2,1,0:T(2,128)S(1)}, u32[]{:S(2)}, u32[]{:S(2)}) %collective-permute-start.7) | collective-permute-done | bytes 262176 | tf_op jit(solution)/shard_map/ppermute | solution.py:10
  164.1 14.8 %collective-permute-done.5 = f32[256,2,128]{2,1,0:T(2,128)S(1)} collective-permute-done((f32[256,2,128]{2,1,0:T(2,128)S(1)}, f32[256,2,128]{2,1,0:T(2,128)S(1)}, u32[]{:S(2)}, u32[]{:S(2)}) %collective-permute-start.5) | collective-permute-done | bytes 262176 | tf_op jit(solution)/shard_map/ppermute | solution.py:10
  (70 shorter events, 34.4 us)
Async XLA Ops:
  0.6 25.1 %copy-start.7 = (bf16[256,2,128]{2,1,0:T(2,128)(2,1)S(1)}, bf16[256,2,128]{2,1,0:T(2,128)(2,1)}, u32[]{:S(2)}) copy-start(bf16[256,2,128]{2,1,0:T(2,128)(2,1)} %param.7) | copy-start | bytes 393220
  0.6 33.9 %copy-start.8 = (bf16[256,2,128]{2,1,0:T(2,128)(2,1)S(1)}, bf16[256,2,128]{2,1,0:T(2,128)(2,1)}, u32[]{:S(2)}) copy-start(bf16[256,2,128]{2,1,0:T(2,128)(2,1)} %param.8) | copy-start | bytes 393220
  3.6 18.7 %all-to-all-start.1 = ((bf16[64,64,128]{2,0,1:T(8,128)(2,1)}), bf16[64,64,128]{2,0,1:T(8,128)(2,1)S(1)}, u32[]{:S(2)}, u32[]{:S(2)}) async-start(bf16[64,64,128]{2,0,1:T(8,128)(2,1)} %copy.55), calls=%async_computation.1 | async-start | bytes 2097152 | tf_op jit(solution)/shard_map/all_to_all | solution.py:82
  22.2 23.3 %all-to-all-start = ((bf16[4,64,16,128]{3,2,1,0:T(8,128)(2,1)}), bf16[4,64,16,128]{3,2,1,0:T(8,128)(2,1)S(1)}, u32[]{:S(2)}, u32[]{:S(2)}) async-start(bf16[4,64,16,128]{3,2,1,0:T(8,128)(2,1)} %pad_maximum_fusion), calls=%async_computation | async-start | bytes 2097152 | tf_op jit(solution)/shard_map/all_to_all | solution.py:71
  25.8 17.0 %collective-permute-start = (bf16[256,2,128]{2,0,1:T(8,128)(2,1)S(1)}, bf16[256,2,128]{2,0,1:T(8,128)(2,1)S(1)}, u32[]{:S(2)}, u32[]{:S(2)}) collective-permute-start(bf16[256,2,128]{2,0,1:T(8,128)(2,1)S(1)} %copy.48), channel_id=1, source_target_pairs={{0,8},{4,12},{8,16},{12,20},{16,24},{20,28},{1,9},{5,13},{9,17},{1... | collective-permute-start | bytes 393224 | tf_op jit(solution)/shard_map/ppermute | solution.py:10
  31.0 11.7 %collective-permute-start.1 = (bf16[256,2,128]{2,0,1:T(8,128)(2,1)S(1)}, bf16[256,2,128]{2,0,1:T(8,128)(2,1)S(1)}, u32[]{:S(2)}, u32[]{:S(2)}) collective-permute-start(bf16[256,2,128]{2,0,1:T(8,128)(2,1)S(1)} %copy.48), channel_id=1, source_target_pairs={{0,4},{4,8},{8,12},{12,16},{16,20},{20,24},{24,28},{1,5},{5,9},{9,... | collective-permute-start | bytes 393224 | tf_op jit(solution)/shard_map/ppermute | solution.py:10
  34.6 9.0 %collective-permute-start.2 = (bf16[256,2,128]{2,0,1:T(8,128)(2,1)S(1)}, bf16[256,2,128]{2,0,1:T(8,128)(2,1)S(1)}, u32[]{:S(2)}, u32[]{:S(2)}) collective-permute-start(bf16[256,2,128]{2,0,1:T(8,128)(2,1)S(1)} %copy.52), channel_id=1, source_target_pairs={{0,8},{4,12},{8,16},{12,20},{16,24},{20,28},{1,9},{5,13},{9,17},{1... | collective-permute-start | bytes 393224 | tf_op jit(solution)/shard_map/ppermute | solution.py:10
  37.8 6.9 %collective-permute-start.3 = (bf16[256,2,128]{2,0,1:T(8,128)(2,1)S(1)}, bf16[256,2,128]{2,0,1:T(8,128)(2,1)S(1)}, u32[]{:S(2)}, u32[]{:S(2)}) collective-permute-start(bf16[256,2,128]{2,0,1:T(8,128)(2,1)S(1)} %copy.52), channel_id=1, source_target_pairs={{0,4},{4,8},{8,12},{12,16},{16,20},{20,24},{24,28},{1,5},{5,9},{9,... | collective-permute-start | bytes 393224 | tf_op jit(solution)/shard_map/ppermute | solution.py:10
  45.9 10.7 %copy-start.1 = (bf16[2,256,8,128]{3,1,2,0:T(8,128)(2,1)}, bf16[2,256,8,128]{3,1,2,0:T(8,128)(2,1)S(1)}, u32[]{:S(2)}) copy-start(bf16[2,256,8,128]{3,1,2,0:T(8,128)(2,1)S(1)} %get-tuple-element.222) | copy-start | bytes 3145732 | tf_op jit(solution)/shard_map/while
  45.9 10.7 %copy-start.3 = (bf16[2,256,8,128]{3,1,2,0:T(8,128)(2,1)}, bf16[2,256,8,128]{3,1,2,0:T(8,128)(2,1)S(1)}, u32[]{:S(2)}) copy-start(bf16[2,256,8,128]{3,1,2,0:T(8,128)(2,1)S(1)} %get-tuple-element.224) | copy-start | bytes 3145732 | tf_op jit(solution)/shard_map/while
  52.5 4.7 %copy-start = (f32[8,256,768]{1,2,0:T(8,128)S(1)}, f32[8,256,768]{1,2,0:T(8,128)}, u32[]{:S(2)}) copy-start(f32[8,256,768]{1,2,0:T(8,128)} %get-tuple-element.187) | copy-start | bytes 18874372 | tf_op jit(solution)/shard_map/while
  73.3 4.0 %copy-start.5 = (f32[2,768,128]{2,0,1:T(2,128)S(1)}, f32[2,768,128]{2,0,1:T(2,128)}, u32[]{:S(2)}) copy-start(f32[2,768,128]{2,0,1:T(2,128)} %get-tuple-element.207) | copy-start | bytes 2359300 | tf_op jit(solution)/shard_map/while
  73.3 13.4 %copy-start.2 = (bf16[2,256,8,128]{3,1,2,0:T(8,128)(2,1)S(1)}, bf16[2,256,8,128]{3,1,2,0:T(8,128)(2,1)}, u32[]{:S(2)}) copy-start(bf16[2,256,8,128]{3,1,2,0:T(8,128)(2,1)} %copy-done.1) | copy-start | bytes 3145732 | tf_op jit(solution)/shard_map/while
  73.3 13.4 %copy-start.4 = (bf16[2,256,8,128]{3,1,2,0:T(8,128)(2,1)S(1)}, bf16[2,256,8,128]{3,1,2,0:T(8,128)(2,1)}, u32[]{:S(2)}) copy-start(bf16[2,256,8,128]{3,1,2,0:T(8,128)(2,1)} %copy-done.3) | copy-start | bytes 3145732 | tf_op jit(solution)/shard_map/while
  86.8 10.7 %copy-start.1 = (bf16[2,256,8,128]{3,1,2,0:T(8,128)(2,1)}, bf16[2,256,8,128]{3,1,2,0:T(8,128)(2,1)S(1)}, u32[]{:S(2)}) copy-start(bf16[2,256,8,128]{3,1,2,0:T(8,128)(2,1)S(1)} %get-tuple-element.222) | copy-start | bytes 3145732 | tf_op jit(solution)/shard_map/while
  86.8 10.7 %copy-start.3 = (bf16[2,256,8,128]{3,1,2,0:T(8,128)(2,1)}, bf16[2,256,8,128]{3,1,2,0:T(8,128)(2,1)S(1)}, u32[]{:S(2)}) copy-start(bf16[2,256,8,128]{3,1,2,0:T(8,128)(2,1)S(1)} %get-tuple-element.224) | copy-start | bytes 3145732 | tf_op jit(solution)/shard_map/while
  93.4 4.7 %copy-start = (f32[8,256,768]{1,2,0:T(8,128)S(1)}, f32[8,256,768]{1,2,0:T(8,128)}, u32[]{:S(2)}) copy-start(f32[8,256,768]{1,2,0:T(8,128)} %get-tuple-element.187) | copy-start | bytes 18874372 | tf_op jit(solution)/shard_map/while
  114.2 13.4 %copy-start.2 = (bf16[2,256,8,128]{3,1,2,0:T(8,128)(2,1)S(1)}, bf16[2,256,8,128]{3,1,2,0:T(8,128)(2,1)}, u32[]{:S(2)}) copy-start(bf16[2,256,8,128]{3,1,2,0:T(8,128)(2,1)} %copy-done.1) | copy-start | bytes 3145732 | tf_op jit(solution)/shard_map/while
  114.2 13.4 %copy-start.4 = (bf16[2,256,8,128]{3,1,2,0:T(8,128)(2,1)S(1)}, bf16[2,256,8,128]{3,1,2,0:T(8,128)(2,1)}, u32[]{:S(2)}) copy-start(bf16[2,256,8,128]{3,1,2,0:T(8,128)(2,1)} %copy-done.3) | copy-start | bytes 3145732 | tf_op jit(solution)/shard_map/while
  130.3 50.5 %all-to-all-start.2 = ((bf16[256,16,128]{2,1,0:T(8,128)(2,1)}), bf16[256,16,128]{2,1,0:T(8,128)(2,1)S(1)}, u32[]{:S(2)}, u32[]{:S(2)}) async-start(bf16[256,16,128]{2,1,0:T(8,128)(2,1)} %bitcast.13), calls=%async_computation.2 | async-start | bytes 2097152 | tf_op jit(solution)/shard_map/all_to_all | solution.py:96
  134.9 14.3 %collective-permute-start.6 = (f32[256,2,128]{2,1,0:T(2,128)S(1)}, f32[256,2,128]{2,1,0:T(2,128)S(1)}, u32[]{:S(2)}, u32[]{:S(2)}) collective-permute-start(f32[256,2,128]{2,1,0:T(2,128)S(1)} %get-tuple-element.112), channel_id=1, source_target_pairs={{4,0},{8,4},{12,8},{16,12},{20,16},{24,20},{28,24},{5,1},{9,5},{13... | collective-permute-start | bytes 786440 | tf_op jit(solution)/shard_map/ppermute | solution.py:10
  136.2 26.2 %collective-permute-start.7 = (f32[256,2,128]{2,1,0:T(2,128)S(1)}, f32[256,2,128]{2,1,0:T(2,128)S(1)}, u32[]{:S(2)}, u32[]{:S(2)}) collective-permute-start(f32[256,2,128]{2,1,0:T(2,128)S(1)} %get-tuple-element.113), channel_id=1, source_target_pairs={{8,0},{12,4},{16,8},{20,12},{24,16},{28,20},{9,1},{13,5},{17,9},{2... | collective-permute-start | bytes 786440 | tf_op jit(solution)/shard_map/ppermute | solution.py:10
  138.5 25.6 %collective-permute-start.4 = (f32[256,2,128]{2,1,0:T(2,128)S(1)}, f32[256,2,128]{2,1,0:T(2,128)S(1)}, u32[]{:S(2)}, u32[]{:S(2)}) collective-permute-start(f32[256,2,128]{2,1,0:T(2,128)S(1)} %get-tuple-element.114), channel_id=1, source_target_pairs={{4,0},{8,4},{12,8},{16,12},{20,16},{24,20},{28,24},{5,1},{9,5},{13... | collective-permute-start | bytes 786440 | tf_op jit(solution)/shard_map/ppermute | solution.py:10
  139.8 39.1 %collective-permute-start.5 = (f32[256,2,128]{2,1,0:T(2,128)S(1)}, f32[256,2,128]{2,1,0:T(2,128)S(1)}, u32[]{:S(2)}, u32[]{:S(2)}) collective-permute-start(f32[256,2,128]{2,1,0:T(2,128)S(1)} %get-tuple-element.115), channel_id=1, source_target_pairs={{8,0},{12,4},{16,8},{20,12},{24,16},{28,20},{9,1},{13,5},{17,9},{2... | collective-permute-start | bytes 786440 | tf_op jit(solution)/shard_map/ppermute | solution.py:10
  (3 other events, 5.7 us)
